TPU v7x, 32 devices: a whole 2x2x4 slice. The times are simulated.
32 devices in a mesh: dp: 8 (over y, x, core), tensor: 4 (over z).
Axes of the slice: x: 2, y: 2, z: 4, core: 2. Of those that a mesh axis runs over, the one named last changes fastest.
Arguments:
- tokens: bfloat16 [128, 8192], P('dp'), may hold values from -6 to 6
- norm_gain: bfloat16 [8192], replicated, may hold values from 0.099609375 to 1.8984375
- w_query: bfloat16 [8192, 8192], P('dp', 'tensor'), may hold values from -0.0625 to 0.0625
- w_key: bfloat16 [8192, 1024], P('dp', 'tensor'), may hold values from -0.0625 to 0.0625
- w_value: bfloat16 [8192, 1024], P('dp', 'tensor'), may hold values from -0.0625 to 0.0625
- check_column: bfloat16 [8192], replicated, may hold values from -6 to 6
- key_cache: bfloat16 [4096, 16, 8, 128], P('dp', None, 'tensor'), may hold values from -320 to 320
- value_cache: bfloat16 [4096, 16, 8, 128], P('dp', None, 'tensor'), may hold values from -6 to 6
- page_table: int32 [128, 32], P('dp'), may hold values from 0 to 511, as said below
- lengths: int32 [128], P('dp'), may hold values from 1 to 512, as said below
- tol_counts: int32 [128], replicated, may hold values from 0 to 7
Outputs:
- attention: bfloat16 [128, 8192], P('dp', 'tensor')
- excess: float32 [], replicated
Inputs may be any that keep to these rules, and one draw needn't show every extreme that they name: page_table holds pool pages of the index of dp that holds the sequence; the 16 sequences of one index of dp own distinct pages and together own all 512 of them. `lengths`: some sequence holds exactly 512 cached tokens.
All inputs are finite; a program needn't handle non-finite values.
Results may differ from a plain program's by a relative error of at most 0.007.
The roundings to bfloat16 on the way count: a program that leaves them out, or rounds other values in their place, can miss the bound.
Values may be sent and summed in bfloat16 or wider, within the bound.
A program may use at most 64 MiB of HBM per device.

v0:
```python
import math
import jax
import jax.numpy as jnp
from jax import lax
from jax.sharding import PartitionSpec as P

HQ = 64
KVH = 8
HD = 128
epsilon = 1e-06
rope_base = 1000000.0
tol_step = 0.25


def normalize(tokens, norm_gain):
    widened = tokens.astype(jnp.float32)
    mean_square = jnp.mean(widened * widened, axis=1, keepdims=True)
    return (widened * lax.rsqrt(mean_square + epsilon) * norm_gain.astype(jnp.float32)).astype(
        jnp.bfloat16
    )


def rotate(vectors, positions):
    half_width = vectors.shape[-1] // 2
    steps_index = jnp.arange(half_width, dtype=jnp.float32)
    inverse = rope_base ** (-2.0 * steps_index / vectors.shape[-1])
    angles = positions.astype(jnp.float32)[:, None] * inverse[None, :]
    cosine = jnp.cos(angles)[:, None, :]
    sine_part = jnp.sin(angles)[:, None, :]
    lower = vectors[..., :half_width]
    upper = vectors[..., half_width:]
    return jnp.concatenate(
        [lower * cosine - upper * sine_part, upper * cosine + lower * sine_part], axis=-1
    )


def attend(query_heads, cached_keys, cached_values, key_new, value_new, lengths):
    score_scale = query_heads.shape[-1] ** (-0.5)
    scores = (
        jnp.einsum("skgd,sckd->skgc", query_heads, cached_keys, preferred_element_type=jnp.float32)
        * score_scale
    )
    new_score = (
        jnp.einsum("skgd,skd->skg", query_heads, key_new, preferred_element_type=jnp.float32)
        * score_scale
    )
    live_mask = (jnp.arange(cached_keys.shape[1])[None, :] < lengths[:, None])[:, None, None, :]
    masked = jnp.where(live_mask, scores, -jnp.inf)
    peak_score = jnp.maximum(jnp.max(masked, axis=-1), new_score)
    weights = jnp.exp(masked - peak_score[..., None])
    new_weight = jnp.exp(new_score - peak_score)
    denominator = jnp.sum(weights, axis=-1) + new_weight
    rounded_new = lax.optimization_barrier(new_weight.astype(jnp.bfloat16)).astype(jnp.float32)
    mixed_heads = jnp.einsum(
        "skgc,sckd->skgd",
        weights.astype(jnp.bfloat16),
        cached_values,
        preferred_element_type=jnp.float32,
    )
    mixed_heads = (
        mixed_heads + rounded_new[..., None] * value_new.astype(jnp.float32)[:, :, None, :]
    )
    return mixed_heads / denominator[..., None]


def body(
    tokens,
    norm_gain,
    w_query,
    w_key,
    w_value,
    check_column,
    key_cache,
    value_cache,
    page_table,
    lengths,
    tol_counts,
):
    seq_rows = tokens.shape[0]
    head_size = key_cache.shape[-1]
    normed = normalize(tokens, norm_gain)
    spread = lax.all_to_all(normed, "dp", split_axis=1, concat_axis=0, tiled=True)
    projected = lax.psum_scatter(
        jnp.concatenate(
            [
                jnp.dot(spread, w_query, preferred_element_type=jnp.float32),
                jnp.dot(spread, w_key, preferred_element_type=jnp.float32),
                jnp.dot(spread, w_value, preferred_element_type=jnp.float32),
            ],
            axis=1,
        ),
        "dp",
        scatter_dimension=0,
        tiled=True,
    )
    column_count = (HQ + 2 * KVH) * HD
    local_sums = jnp.sum(projected, axis=1)
    check_sums = jnp.dot(normed, check_column, preferred_element_type=jnp.float32)
    all_rows = seq_rows * lax.axis_size("dp")
    block_total = lax.psum(local_sums, "tensor")
    residual = (block_total - check_sums) / math.sqrt(column_count)
    own_counts = lax.dynamic_slice_in_dim(tol_counts, lax.axis_index("dp") * seq_rows, seq_rows, 0)
    token_excess = jnp.maximum(jnp.abs(residual) - tol_step * own_counts.astype(jnp.float32), 0.0)
    excess = lax.psum(jnp.sum(token_excess), "dp") / math.sqrt(all_rows)
    query_width = w_query.shape[1]
    kv_width = w_key.shape[1]
    heads_here = query_width // head_size
    kv_here = kv_width // head_size
    group_size = heads_here // kv_here
    query_heads = rotate(
        projected[:, :query_width].reshape(seq_rows, heads_here, head_size), lengths
    ).astype(jnp.bfloat16)
    key_new = rotate(
        projected[:, query_width : query_width + kv_width].reshape(seq_rows, kv_here, head_size),
        lengths,
    ).astype(jnp.bfloat16)
    value_new = (
        projected[:, query_width + kv_width :]
        .reshape(seq_rows, kv_here, head_size)
        .astype(jnp.bfloat16)
    )
    context = page_table.shape[1] * key_cache.shape[1]
    cached_keys = key_cache[page_table].reshape(seq_rows, context, kv_here, head_size)
    cached_values = value_cache[page_table].reshape(seq_rows, context, kv_here, head_size)
    mixed_heads = attend(
        query_heads.reshape(seq_rows, kv_here, group_size, head_size),
        cached_keys,
        cached_values,
        key_new,
        value_new,
        lengths,
    )
    attention = mixed_heads.reshape(seq_rows, heads_here * head_size).astype(jnp.bfloat16)
    return (attention, excess)


def solution(mesh):
    return jax.shard_map(
        body,
        mesh=mesh,
        in_specs=(
            P("dp", None),
            P(),
            P("dp", "tensor"),
            P("dp", "tensor"),
            P("dp", "tensor"),
            P(),
            P("dp", None, "tensor", None),
            P("dp", None, "tensor", None),
            P("dp", None),
            P("dp"),
            P(),
        ),
        out_specs=(P("dp", "tensor"), P()),
        check_vma=False,
    )
```

profile of v0, /device:TPU:0, one launch (start us, length us, event | category | flops | bytes accessed | tf_op | source)
XLA Modules:
  0.0 112.8 jit_solution(3940813790565365840)
XLA Ops:
  7.2 0.0 copy-start
  7.2 0.0 reduce-scatter.2.cloned.1.call-start
  7.2 0.8 convert_element_type.51
  8.0 1.1 fusion.25
  9.2 1.1 fusion.27
  10.3 11.9 %all_to_all.19 = bf16[16,8,1024]{2,0,1:T(8,128)(2,1)S(1)} all-to-all(bf16[16,8,1024]{2,0,1:T(8,128)(2,1)S(1)} %bitcast.54), channel_id=1, replica_groups=mesh['dp'=8,'tensor'=4] {'dp'}, dimensions={1} | all-to-all | bytes 524288 | tf_op jit(solution)/shard_map/all_to_all | solution.py:82
  22.2 2.9 %fusion.42 = f32[128,2048]{1,0:T(8,128)S(1)} fusion(bf16[128,1024]{1,0:T(8,128)(2,1)S(1)} %bitcast.49, bf16[1024,2048]{1,0:T(8,128)(2,1)} %param.13), kind=kOutput, calls=%fused_computation.57 | convolution fusion | flops 536870912 | bytes 5505024 | tf_op jit(solution)/shard_map/dot_general | solution.py:86
  25.1 0.2 fusion.43
  25.4 0.2 fusion.44
  25.7 1.3 %pad_maximum_fusion = f32[128,2560]{1,0:T(8,128)} fusion(f32[128,256]{1,0:T(8,128)S(1)} %fusion.44, f32[128,256]{1,0:T(8,128)S(1)} %fusion.43, f32[128,2048]{1,0:T(8,128)S(1)} %fusion.42), kind=kLoop, calls=%fused_computation.6 | loop fusion | flops 655360 | bytes 2621440 | tf_op jit(solution)/shard_map/concatenate | solution.py:84
  26.9 0.0 reduce-scatter.2.cloned.1.call-update
  27.0 0.1 reshape.122
  27.1 20.9 %gather_fusion = bf16[512,16,2,128]{3,2,1,0:T(2,128)(2,1)} fusion(bf16[512,16,2,128]{3,2,1,0:T(2,128)(2,1)} %param.17, s32[1024]{0:T(1024)S(1)} %pad_clamp_fusion), kind=kCustom, calls=%fused_computation | custom fusion | bytes 8390656 | tf_op jit(solution)/shard_map/gather | solution.py:123
  47.9 20.9 %gather_fusion.1 = bf16[512,16,2,128]{3,2,1,0:T(2,128)(2,1)} fusion(bf16[512,16,2,128]{3,2,1,0:T(2,128)(2,1)} %param.18, s32[1024]{0:T(1024)S(1)} %pad_clamp_fusion), kind=kCustom, calls=%fused_computation.1 | custom fusion | bytes 8390656 | tf_op jit(solution)/shard_map/gather | solution.py:124
  68.9 0.1 iota_compare_fusion
  68.9 0.1 multiply_cosine_fusion
  69.1 0.0 reduce-scatter.2.cloned.1.call-done
  69.1 0.8 slice.36
  69.9 0.9 slice_bitcast_fusion
  70.9 0.1 subtract_convert_fusion.1
  71.0 0.1 fusion.32
  71.1 0.1 maximum_bitcast_fusion
  71.2 0.2 fusion.34
  71.4 3.5 %fusion.41 = (f32[16,2,8]{2,1,0:T(2,128)S(1)}, f32[16,2,8,512]{3,2,1,0:T(8,128)S(1)}) fusion(bf16[16,512,2,128]{3,2,1,0:T(2,128)(2,1)} %bitcast.47, bf16[16,2,8,64]{3,2,1,0:T(8,128)(2,1)S(1)} %get-tuple-element.3, bf16[16,2,8,64]{3,2,1,0:T(8,128)(2,1)S(1)} %get-tuple-element.2, pred[16,512]{1,0:T(8,128)(4,1)S(1)} %iota_compare_fusion), kind=kOutput, calls=%fused_computation.56 | convolution fusion | flops 34078464 | bytes 4793344 | tf_op jit(solution)/shard_map/skgd,sckd->skgc/dot_general | solution.py:40
  74.9 0.0 copy-start.6
  74.9 0.2 fusion.28
  75.3 0.1 reduce_sum.38
  75.4 12.0 %psum.14 = f32[16]{0:T(128)S(1)} all-reduce(f32[16]{0:T(128)S(1)} %reduce_sum.38), channel_id=1, replica_groups=mesh['dp'=8,'tensor'=4] {'tensor'}, use_global_device_ids=true, to_apply=%region_5.0 | all-reduce | flops 16 | bytes 128 | tf_op jit(solution)/shard_map/psum | solution.py:100
  87.4 2.9 %fusion.16 = bf16[16,2,8,128]{3,2,1,0:T(8,128)(2,1)S(1)} fusion(bf16[16,512,2,128]{3,2,1,0:T(2,128)(2,1)} %bitcast.48, f32[16,2,8,512]{3,2,1,0:T(8,128)S(1)} %get-tuple-element.11, f32[16,2,8]{2,1,0:T(2,128)S(1)} %multiply_maximum_fusion, f32[16,2,8]{2,1,0:T(2,128)S(1)} %get-tuple-element.5, f32[16,2,128]{2,1,0:T(2,128)S(1)} %reshape.119, ...), kind=kOutput, calls=%fused_computation.11 | convolution fusion | flops 33947648 | bytes 4803584 | tf_op jit(solution)/shard_map/skgc,sckd->skgd/dot_general | solution.py:54
  90.3 0.8 fusion.24
  91.1 0.6 copy.49
  91.7 12.4 %psum.15 = f32[]{:T(128)} all-reduce(f32[]{:T(128)} %fusion.24), channel_id=1, replica_groups=mesh['dp'=8,'tensor'=4] {'dp'}, use_global_device_ids=true, to_apply=%region_7.8 | all-reduce | flops 1 | bytes 8 | tf_op jit(solution)/shard_map/psum | solution.py:104
  (26 shorter events, 0.2 us)
Async XLA Ops:
  7.2 18.0 %copy-start = (bf16[1024,256]{1,0:T(8,128)(2,1)S(1)}, bf16[1024,256]{1,0:T(8,128)(2,1)}, u32[]{:S(2)}) copy-start(bf16[1024,256]{1,0:T(8,128)(2,1)} %param.14) | copy-start | bytes 1572868
  7.2 18.2 %copy-start.2 = (bf16[1024,256]{1,0:T(8,128)(2,1)S(1)}, bf16[1024,256]{1,0:T(8,128)(2,1)}, u32[]{:S(2)}) copy-start(bf16[1024,256]{1,0:T(8,128)(2,1)} %param.15) | copy-start | bytes 1572868
  7.2 61.9 %reduce-scatter.2.cloned.1.call-start = ((), (), s32[]{:S(2)}) async-start(), calls=%async_computation.2 | async-start | bytes 1474560 | tf_op jit(solution)/shard_map/reduce_scatter | solution.py:83
  25.1 1.8 %copy-start.5 = (s32[16]{0:T(128)S(1)}, s32[16]{0:T(128)}, u32[]{:S(2)}) copy-start(s32[16]{0:T(128)} %param.20) | copy-start | bytes 196
  25.1 1.8 %copy-start.4 = (s32[16,32]{1,0:T(8,128)S(1)}, s32[16,32]{1,0:T(8,128)}, u32[]{:S(2)}) copy-start(s32[16,32]{1,0:T(8,128)} %param.19) | copy-start | bytes 6148
  47.9 20.9 %copy-start.3 = (bf16[8192]{0:T(1024)(128)(2,1)S(1)}, bf16[8192]{0:T(1024)(128)(2,1)}, u32[]{:S(2)}) copy-start(bf16[8192]{0:T(1024)(128)(2,1)} %param.16) | copy-start | bytes 49156
  69.1 6.1 %copy-start.1 = (f32[16,2560]{1,0:T(8,128)S(1)}, f32[16,2560]{1,0:T(8,128)}, u32[]{:S(2)}) copy-start(f32[16,2560]{1,0:T(8,128)} %reduce-scatter.2.cloned.1.call-done) | copy-start | bytes 491524
  74.9 15.4 %copy-start.6 = (s32[128]{0:T(128)S(1)}, s32[128]{0:T(128)}, u32[]{:S(2)}) copy-start(s32[128]{0:T(128)} %param.21) | copy-start | bytes 1540
Sparse Core Ops, SparseCore 0:
  27.1 36.5 reduce-scatter.1
where the time goes:
time: 113 us
  local copies, waits for them, and re-layouts  44.3 us (39%)
  blocking collectives  36.3 us (32%)
  between operations  16.1 us (14%)
  matrix products  10.8 us (10%)
  other arithmetic  5.21 us (5%)
    gather x1, local copies, waits for them, and re-layouts, body(): value_cache[page_table].reshape(seq_rows, context, kv_here, head_size)  20.9 us
    gather x1, local copies, waits for them, and re-layouts, body(): key_cache[page_table].reshape(seq_rows, context, kv_here, head_size)  20.9 us
    psum x1, blocking collectives, body(): excess = lax.psum(jnp.sum(token_excess), 'dp') / math.sqrt(all_rows)  12.4 us
    psum x1, blocking collectives, body(): block_total = lax.psum(local_sums, 'tensor')  12 us
    all_to_all x1, blocking collectives, body(): lax.all_to_all(normed, 'dp', split_axis=1, concat_axis=0, tiled=True)  11.9 us
    dot_general x1, matrix products, attend(): jnp.einsum('skgd,sckd->skgc', query_heads, cached_keys, preferred_element...  3.52 us
    dot_general x1, matrix products, body(): jnp.dot(spread, w_query, preferred_element_type=jnp.float32)  2.92 us
    dot_general x1, matrix products, attend(): jnp.einsum('skgc,sckd->skgd', weights.astype(jnp.bfloat16), cached_values...  2.89 us
  transfers between devices with their start and end apart: 1, of which 0 were waited for; matrix products, arithmetic and copies ran while one was open for 37% of the time, Pallas kernels for 0%

commit v1 on v0

--- a/solution.py
+++ b/solution.py
@@ -3,6 +3,7 @@
 import jax.numpy as jnp
 from jax import lax
 from jax.sharding import PartitionSpec as P
+from jax.lax import all_gather
 
 HQ = 64
 KVH = 8
@@ -97,7 +98,11 @@
     local_sums = jnp.sum(projected, axis=1)
     check_sums = jnp.dot(normed, check_column, preferred_element_type=jnp.float32)
     all_rows = seq_rows * lax.axis_size("dp")
-    block_total = lax.psum(local_sums, "tensor")
+
+    def place_the_scenes(in_array):
+        return all_gather(in_array, "tensor").sum(axis=0)
+
+    block_total = place_the_scenes(local_sums)
     residual = (block_total - check_sums) / math.sqrt(column_count)
     own_counts = lax.dynamic_slice_in_dim(tol_counts, lax.axis_index("dp") * seq_rows, seq_rows, 0)
     token_excess = jnp.maximum(jnp.abs(residual) - tol_step * own_counts.astype(jnp.float32), 0.0)

time: 113 us -> 115 us (1.018)
    psum x1 -> x0, blocking collectives: 12 us -> none  [body(): block_total = lax.psum(local_sums, 'tensor')]
    unnamed x0 -> x1, blocking collectives: none -> 11.9 us
    unnamed x18 -> x23, local copies, waits for them, and re-layouts: 1.65 us -> 2.48 us
where the time goes in v1:
time: 115 us; the launch traced here: 114 us
  local copies, waits for them, and re-layouts  45.2 us (39%)
  blocking collectives  36.3 us (32%)
  between operations  16.7 us (15%)
  matrix products  10.8 us (9%)
  other arithmetic  5.24 us (5%)
    gather x1, local copies, waits for them, and re-layouts, body(): value_cache[page_table].reshape(seq_rows, context, kv_here, head_size)  20.9 us
    gather x1, local copies, waits for them, and re-layouts, body(): key_cache[page_table].reshape(seq_rows, context, kv_here, head_size)  20.9 us
    psum x1, blocking collectives, body(): excess = lax.psum(jnp.sum(token_excess), 'dp') / math.sqrt(all_rows)  12.4 us
    unnamed x1, blocking collectives  11.9 us
    all_to_all x1, blocking collectives, body(): lax.all_to_all(normed, 'dp', split_axis=1, concat_axis=0, tiled=True)  11.9 us
    dot_general x1, matrix products, attend(): jnp.einsum('skgd,sckd->skgc', query_heads, cached_keys, preferred_element...  3.52 us
    dot_general x1, matrix products, body(): jnp.dot(spread, w_query, preferred_element_type=jnp.float32)  2.92 us
    dot_general x1, matrix products, attend(): jnp.einsum('skgc,sckd->skgd', weights.astype(jnp.bfloat16), cached_values...  2.89 us
  transfers between devices with their start and end apart: 1, of which 0 were waited for; matrix products, arithmetic and copies ran while one was open for 37% of the time, Pallas kernels for 0%

profile of v1, /device:TPU:0, one launch (start us, length us, event | category | flops | bytes accessed | tf_op | source)
XLA Modules:
  0.0 114.4 jit_solution(8122586701614347097)
XLA Ops:
  7.2 0.0 reduce-scatter.2.cloned.1.call-start
  7.2 0.8 convert_element_type.51
  8.0 1.1 fusion.25
  9.2 1.1 fusion.27
  10.3 11.9 %all_to_all.19 = bf16[16,8,1024]{2,0,1:T(8,128)(2,1)S(1)} all-to-all(bf16[16,8,1024]{2,0,1:T(8,128)(2,1)S(1)} %bitcast.55), channel_id=1, replica_groups=mesh['dp'=8,'tensor'=4] {'dp'}, dimensions={1} | all-to-all | bytes 524288 | tf_op jit(solution)/shard_map/all_to_all | solution.py:83
  22.2 2.9 %fusion.42 = f32[128,2048]{1,0:T(8,128)S(1)} fusion(bf16[128,1024]{1,0:T(8,128)(2,1)S(1)} %bitcast.50, bf16[1024,2048]{1,0:T(8,128)(2,1)} %param.13), kind=kOutput, calls=%fused_computation.57 | convolution fusion | flops 536870912 | bytes 5505024 | tf_op jit(solution)/shard_map/dot_general | solution.py:87
  25.1 0.2 fusion.43
  25.4 0.2 fusion.44
  25.7 1.3 %pad_maximum_fusion = f32[128,2560]{1,0:T(8,128)} fusion(f32[128,256]{1,0:T(8,128)S(1)} %fusion.44, f32[128,256]{1,0:T(8,128)S(1)} %fusion.43, f32[128,2048]{1,0:T(8,128)S(1)} %fusion.42), kind=kLoop, calls=%fused_computation.6 | loop fusion | flops 655360 | bytes 2621440 | tf_op jit(solution)/shard_map/concatenate | solution.py:85
  27.0 0.1 reshape.122
  27.1 20.9 %gather_fusion = bf16[512,16,2,128]{3,2,1,0:T(2,128)(2,1)} fusion(bf16[512,16,2,128]{3,2,1,0:T(2,128)(2,1)} %param.17, s32[1024]{0:T(1024)S(1)} %pad_clamp_fusion), kind=kCustom, calls=%fused_computation | custom fusion | bytes 8390656 | tf_op jit(solution)/shard_map/gather | solution.py:128
  47.9 20.9 %gather_fusion.1 = bf16[512,16,2,128]{3,2,1,0:T(2,128)(2,1)} fusion(bf16[512,16,2,128]{3,2,1,0:T(2,128)(2,1)} %param.18, s32[1024]{0:T(1024)S(1)} %pad_clamp_fusion), kind=kCustom, calls=%fused_computation.1 | custom fusion | bytes 8390656 | tf_op jit(solution)/shard_map/gather | solution.py:129
  68.9 0.6 dynamic-slice
  70.1 0.1 iota_compare_fusion
  70.2 0.1 multiply_cosine_fusion
  70.3 0.0 reduce-scatter.2.cloned.1.call-done
  70.4 0.8 slice.36
  71.2 0.9 slice_bitcast_fusion
  72.1 0.1 subtract_convert_fusion.1
  72.2 0.1 fusion.32
  72.3 0.1 maximum_bitcast_fusion
  72.4 0.2 fusion.34
  72.6 3.5 %fusion.41 = (f32[16,2,8]{2,1,0:T(2,128)S(1)}, f32[16,2,8,512]{3,2,1,0:T(8,128)S(1)}) fusion(bf16[16,512,2,128]{3,2,1,0:T(2,128)(2,1)} %bitcast.48, bf16[16,2,8,64]{3,2,1,0:T(8,128)(2,1)S(1)} %get-tuple-element.3, bf16[16,2,8,64]{3,2,1,0:T(8,128)(2,1)S(1)} %get-tuple-element.2, pred[16,512]{1,0:T(8,128)(4,1)S(1)} %iota_compare_fusion), kind=kOutput, calls=%fused_computation.56 | convolution fusion | flops 34078464 | bytes 4793344 | tf_op jit(solution)/shard_map/skgd,sckd->skgc/dot_general | solution.py:41
  76.2 0.2 fusion.28
  76.5 0.1 reduce_sum.47
  76.7 0.2 dynamic-update-slice
  76.9 11.9 %all-reduce = f32[64]{0:T(128)S(1)} all-reduce(f32[64]{0:T(128)S(1)} %dynamic-update-slice), channel_id=2, replica_groups=mesh['dp'=8,'tensor'=4] {'tensor'}, use_global_device_ids=true, to_apply=%add | all-reduce | flops 64 | bytes 512
  88.9 0.1 reshape.136
  89.0 2.9 %fusion.16 = bf16[16,2,8,128]{3,2,1,0:T(8,128)(2,1)S(1)} fusion(bf16[16,512,2,128]{3,2,1,0:T(2,128)(2,1)} %bitcast.49, f32[16,2,8,512]{3,2,1,0:T(8,128)S(1)} %get-tuple-element.11, f32[16,2,8]{2,1,0:T(2,128)S(1)} %multiply_maximum_fusion, f32[16,2,8]{2,1,0:T(2,128)S(1)} %get-tuple-element.5, f32[16,2,128]{2,1,0:T(2,128)S(1)} %reshape.119, ...), kind=kOutput, calls=%fused_computation.11 | convolution fusion | flops 33947648 | bytes 4803584 | tf_op jit(solution)/shard_map/skgc,sckd->skgd/dot_general | solution.py:55
  91.9 0.8 fusion.24
  92.7 0.6 copy.49
  93.3 12.4 %psum.7 = f32[]{:T(128)} all-reduce(f32[]{:T(128)} %fusion.24), channel_id=1, replica_groups=mesh['dp'=8,'tensor'=4] {'dp'}, use_global_device_ids=true, to_apply=%region_7.8 | all-reduce | flops 1 | bytes 8 | tf_op jit(solution)/shard_map/psum | solution.py:109
  (33 shorter events, 0.3 us)
Async XLA Ops:
  7.2 18.0 %copy-start = (bf16[1024,256]{1,0:T(8,128)(2,1)S(1)}, bf16[1024,256]{1,0:T(8,128)(2,1)}, u32[]{:S(2)}) copy-start(bf16[1024,256]{1,0:T(8,128)(2,1)} %param.14) | copy-start | bytes 1572868
  7.2 18.2 %copy-start.2 = (bf16[1024,256]{1,0:T(8,128)(2,1)S(1)}, bf16[1024,256]{1,0:T(8,128)(2,1)}, u32[]{:S(2)}) copy-start(bf16[1024,256]{1,0:T(8,128)(2,1)} %param.15) | copy-start | bytes 1572868
  7.2 63.2 %reduce-scatter.2.cloned.1.call-start = ((), (), s32[]{:S(2)}) async-start(), calls=%async_computation.2 | async-start | bytes 1474560 | tf_op jit(solution)/shard_map/reduce_scatter | solution.py:84
  25.1 1.8 %copy-start.5 = (s32[16]{0:T(128)S(1)}, s32[16]{0:T(128)}, u32[]{:S(2)}) copy-start(s32[16]{0:T(128)} %param.20) | copy-start | bytes 196
  25.1 1.8 %copy-start.4 = (s32[16,32]{1,0:T(8,128)S(1)}, s32[16,32]{1,0:T(8,128)}, u32[]{:S(2)}) copy-start(s32[16,32]{1,0:T(8,128)} %param.19) | copy-start | bytes 6148
  47.9 20.9 %copy-start.3 = (bf16[8192]{0:T(1024)(128)(2,1)S(1)}, bf16[8192]{0:T(1024)(128)(2,1)}, u32[]{:S(2)}) copy-start(bf16[8192]{0:T(1024)(128)(2,1)} %param.16) | copy-start | bytes 49156
  47.9 20.9 %copy-start.7 = (u32[32]{0:T(128)S(1)}, u32[32]{0:T(128)}, u32[]{:S(2)}) copy-start(u32[32]{0:T(128)} %constant.46) | copy-start | bytes 388
  70.4 6.1 %copy-start.1 = (f32[16,2560]{1,0:T(8,128)S(1)}, f32[16,2560]{1,0:T(8,128)}, u32[]{:S(2)}) copy-start(f32[16,2560]{1,0:T(8,128)} %reduce-scatter.2.cloned.1.call-done) | copy-start | bytes 491524
  76.2 15.7 %copy-start.6 = (s32[128]{0:T(128)S(1)}, s32[128]{0:T(128)}, u32[]{:S(2)}) copy-start(s32[128]{0:T(128)} %param.21) | copy-start | bytes 1540
Sparse Core Ops, SparseCore 0:
  27.1 36.5 reduce-scatter.1
